TPU v7x, 256 devices: a whole 4x4x8 slice. The times are simulated.
256 devices in a mesh: dop: 32 (over z, y), slow: 8 (over x, core).
Axes of the slice: x: 4, y: 4, z: 8, core: 2. Of those that a mesh axis runs over, the one named last changes fastest.
Arguments:
- profiles: bfloat16 [64, 2, 1024, 2048], P('slow', None, 'dop'), may hold values from -6 to 6
- range_walk: int32 [2048], replicated, may hold values from -32 to 32
- band_order: int32 [256], replicated, may hold values from 0 to 255, each once
Outputs:
- ambiguity: float32 [2048, 1024], P(('dop', 'slow'))
Inputs may be any that keep to these rules, and one draw needn't show every extreme that they name: `band_order`: each band number appears exactly once.
All inputs are finite; a program needn't handle non-finite values.
Results may differ from a plain program's by a relative error of at most 0.00067.
Values sent between devices are 32-bit elements; how exact they have to be, the bound alone decides.
No kernel may reach another device: no remote copies, remote signals or barrier semaphores. Data moves between devices by JAX's collectives and lax.ppermute only.
A program may use at most 64 MiB of HBM per device.

v0:
```python
import math
import jax
import jax.numpy as jnp
from jax import lax
from jax.sharding import PartitionSpec as P

WALK = 32


def from_behind(value, axis, steps):
    count = lax.axis_size(axis)
    leading, last = (max(0, -steps), min(count, count - steps))
    return lax.ppermute(value, axis, [(source, source + steps) for source in range(leading, last)])


def cut_along(x, dim, devices):
    before, after = (x.shape[:dim], x.shape[dim + 1 :])
    return jnp.moveaxis(x.reshape(*before, devices, -1, *after), dim, 0)


def summed_on_arrival(x, axis, dim):
    tiles = cut_along(x, dim, lax.axis_size(axis))
    arrived = lax.all_to_all(tiles, axis, split_axis=0, concat_axis=0, tiled=True)
    return arrived.sum(axis=0)


def fourier_tables(length):
    counter = jnp.arange(length, dtype=jnp.int32)
    phases = counter[:, None] * counter[None, :] % length
    angles = phases.astype(jnp.float32) * (2.0 * math.pi / length)
    return (jnp.cos(angles).astype(jnp.bfloat16), jnp.sin(angles).astype(jnp.bfloat16))


def batch_powers(block, cosine, sine_table):
    count = block.shape[0]
    delays = block.shape[2]
    bins = block.shape[3]
    stacked = block.reshape(count * 2 * delays, bins)
    first = jnp.dot(stacked, cosine, preferred_element_type=jnp.float32).reshape(
        count, 2, delays, bins
    )
    second = jnp.dot(stacked, sine_table, preferred_element_type=jnp.float32).reshape(
        count, 2, delays, bins
    )
    real_part = first[:, 0] + second[:, 1]
    imag_part = first[:, 1] - second[:, 0]
    return real_part * real_part + imag_part * imag_part


def walk_align(padded, offsets, out_rows, reach):
    moves = offsets + reach
    levels = max(1, (2 * reach).bit_length())
    needed = out_rows + (1 << levels) - 1
    current = jnp.pad(padded, ((0, 0), (0, needed - padded.shape[1]), (0, 0)))
    for level in range(levels):
        stride = 1 << level
        taken = (moves // stride % 2 == 1)[:, None, :]
        current = jnp.where(taken, current[:, stride:], current[:, :-stride])
    return current


def permute_bands(values, band_order, band_count):
    picker = (band_order[:, None] == jnp.arange(band_count, dtype=jnp.int32)[None, :]).astype(
        jnp.float32
    )
    return jnp.einsum("bc,...cj->...bj", picker, values, precision=lax.Precision.HIGHEST)


def on_device(profiles, range_walk, band_order):
    batch_count = profiles.shape[0]
    local_rows = profiles.shape[2]
    doppler_bins = profiles.shape[3]
    dop_count = lax.axis_size("dop")
    slow_count = lax.axis_size("slow")
    total_batches = batch_count * slow_count
    band_count = dop_count * slow_count
    band_rows = doppler_bins // band_count
    scale = 1.0 / (total_batches * doppler_bins)
    cosine, sine_table = fourier_tables(doppler_bins)
    powers = batch_powers(profiles, cosine, sine_table)
    batches = lax.axis_index("slow") * batch_count + jnp.arange(batch_count, dtype=jnp.int32)
    offsets = range_walk[None, :] * batches[:, None] // total_batches
    widened = jnp.pad(powers, ((0, 0), (2 * WALK, 2 * WALK), (0, 0)))
    gathered = jnp.sum(walk_align(widened, offsets, local_rows + 2 * WALK, WALK), axis=0)
    lower_rim = gathered[:WALK]
    upper_rim = gathered[local_rows + WALK :]
    own_rows = gathered[WALK : local_rows + WALK]
    from_below = from_behind(upper_rim, "dop", 1)
    from_above = from_behind(lower_rim, "dop", -1)
    own_rows = own_rows.at[:WALK].add(from_below)
    own_rows = own_rows.at[local_rows - WALK :].add(from_above)
    partial_value = own_rows * scale
    ordered = permute_bands(
        partial_value.reshape(local_rows, band_count, band_rows), band_order, band_count
    )
    grouped = ordered.reshape(local_rows, dop_count, slow_count, band_rows).transpose(0, 2, 1, 3)
    grouped = grouped.reshape(local_rows, doppler_bins)
    summed = summed_on_arrival(grouped, "slow", 1)
    result = lax.all_to_all(summed, "dop", split_axis=1, concat_axis=0, tiled=True)
    return result.T


def solution(mesh):
    placed = (P("slow", None, "dop", None), P(), P())
    return jax.shard_map(
        on_device, mesh=mesh, in_specs=placed, out_specs=P(("dop", "slow"), None), check_vma=False
    )
```

profile of v0, /device:TPU:1, one launch (start us, length us, event | category | flops | bytes accessed | tf_op | source)
XLA Modules:
  0.0 232.3 jit_solution(15600399316770278802)
XLA Ops:
  0.0 1.6 copy-done
  1.6 63.9 %fusion.7 = f32[2048,512]{0,1:T(8,128)} fusion(bf16[512,2048]{1,0:T(8,128)(2,1)S(1)} %bitcast.66), kind=kOutput, calls=%fused_computation.19 | convolution fusion | flops 4357881856 | bytes 6291456 | tf_op jit(solution)/shard_map/dot_general | solution.py:39
  65.5 64.4 %fusion.8 = f32[2048,512]{0,1:T(8,128)} fusion(bf16[512,2048]{1,0:T(8,128)(2,1)S(1)} %bitcast.65), kind=kOutput, calls=%fused_computation.20 | convolution fusion | flops 4357881856 | bytes 6291456 | tf_op jit(solution)/shard_map/dot_general | solution.py:42
  130.4 4.5 %fusion.15 = f32[8,32,2048]{2,1,0:T(8,128)S(1)} fusion(f32[8,2,32,2048]{3,2,1,0:T(8,128)} %bitcast.71, f32[8,2,32,2048]{3,2,1,0:T(8,128)} %bitcast.70), kind=kLoop, calls=%fused_computation.27 | loop fusion | flops 2621440 | bytes 10485760 | tf_op jit(solution)/shard_map/add | solution.py:47
  134.9 7.2 %fusion.6 = f32[8,222,2048]{2,1,0:T(8,128)} fusion(f32[8,32,2048]{2,1,0:T(8,128)S(1)} %fusion.15, pred[8,2048]{1,0:T(8,128)(4,1)S(1)} %get-tuple-element.51), kind=kLoop, calls=%fused_computation.13 | loop fusion | flops 3637248 | bytes 16662528 | tf_op jit(solution)/shard_map/jit(_where)/select_n | solution.py:58
  142.1 10.7 %slice_select_fusion = f32[8,220,2048]{2,1,0:T(8,128)S(1)} fusion(f32[8,222,2048]{2,1,0:T(8,128)} %fusion.6, pred[8,2048]{1,0:T(8,128)(4,1)S(1)} %get-tuple-element.53), kind=kLoop, calls=%fused_computation.14 | loop fusion | flops 3604480 | bytes 43270144 | tf_op jit(solution)/shard_map/jit(_where)/select_n | solution.py:58
  152.8 3.4 %slice_select_fusion.1 = f32[8,216,2048]{2,1,0:T(8,128)S(1)} fusion(f32[8,220,2048]{2,1,0:T(8,128)S(1)} %slice_select_fusion, pred[8,2048]{1,0:T(8,128)(4,1)S(1)} %get-tuple-element.49), kind=kLoop, calls=%fused_computation.15 | loop fusion | flops 3538944 | bytes 42483712 | tf_op jit(solution)/shard_map/jit(_where)/select_n | solution.py:58
  156.2 6.7 %slice_select_fusion.2 = f32[8,208,2048]{2,1,0:T(8,128)} fusion(f32[8,216,2048]{2,1,0:T(8,128)S(1)} %slice_select_fusion.1, pred[8,2048]{1,0:T(8,128)(4,1)S(1)} %get-tuple-element.52), kind=kLoop, calls=%fused_computation.16 | loop fusion | flops 3407872 | bytes 40910848 | tf_op jit(solution)/shard_map/jit(_where)/select_n | solution.py:58
  162.9 9.4 %slice_select_fusion.3 = f32[8,192,2048]{2,1,0:T(8,128)S(1)} fusion(f32[8,208,2048]{2,1,0:T(8,128)} %slice_select_fusion.2, pred[8,2048]{1,0:T(8,128)(4,1)S(1)} %get-tuple-element.50), kind=kLoop, calls=%fused_computation.17 | loop fusion | flops 3145728 | bytes 37765120 | tf_op jit(solution)/shard_map/jit(_where)/select_n | solution.py:58
  172.3 3.7 %slice_select_fusion.4 = f32[8,160,2048]{2,1,0:T(8,128)S(1)} fusion(f32[8,192,2048]{2,1,0:T(8,128)S(1)} %slice_select_fusion.3, pred[8,2048]{1,0:T(8,128)(4,1)S(1)} %get-tuple-element.48), kind=kLoop, calls=%fused_computation.18 | loop fusion | flops 2621440 | bytes 31473664 | tf_op jit(solution)/shard_map/jit(_where)/select_n | solution.py:58
  176.0 1.2 fusion.11
  177.3 4.0 %collective-permute-start = (f32[32,2048]{1,0:T(8,128)S(1)}, f32[32,2048]{1,0:T(8,128)S(1)}, u32[]{:S(2)}, u32[]{:S(2)}) collective-permute-start(f32[32,2048]{1,0:T(8,128)S(1)} %get-tuple-element.45), channel_id=1, source_target_pairs={{0,8},{8,16},{16,24},{24,32},{32,40},{40,48},{48,56},{56,64},{64,7... | collective-permute-start | bytes 786440 | tf_op jit(solution)/shard_map/ppermute | solution.py:13
  181.4 1.3 collective-permute-start.1
  182.7 3.7 %collective-permute-done = f32[32,2048]{1,0:T(8,128)S(1)} collective-permute-done((f32[32,2048]{1,0:T(8,128)S(1)}, f32[32,2048]{1,0:T(8,128)S(1)}, u32[]{:S(2)}, u32[]{:S(2)}) %collective-permute-start) | collective-permute-done | bytes 262176 | tf_op jit(solution)/shard_map/ppermute | solution.py:13
  186.3 3.8 %collective-permute-done.1 = f32[32,2048]{1,0:T(8,128)S(1)} collective-permute-done((f32[32,2048]{1,0:T(8,128)S(1)}, f32[32,2048]{1,0:T(8,128)S(1)}, u32[]{:S(2)}, u32[]{:S(2)}) %collective-permute-start.1) | collective-permute-done | bytes 262176 | tf_op jit(solution)/shard_map/ppermute | solution.py:13
  191.0 1.1 convolution_bitcast_fusion
  192.1 1.4 copy.27
  193.4 1.1 copy.37
  194.5 1.5 copy.29
  196.0 12.4 %all_to_all.24 = f32[8,32,256]{2,1,0:T(8,128)S(1)} all-to-all(f32[8,32,256]{2,1,0:T(8,128)S(1)} %copy.29), channel_id=1, replica_groups=mesh['dop'=32,'slow'=8] {'slow'}, dimensions={0} | all-to-all | bytes 524288 | tf_op jit(solution)/shard_map/all_to_all | solution.py:23
  208.7 21.5 %all_to_all.25 = f32[32,1,256]{2,1,0:T(1,128)S(1)} all-to-all(f32[32,1,256]{2,1,0:T(1,128)S(1)} %reshape.392), channel_id=1, replica_groups=mesh['dop'=32,'slow'=8] {'dop'}, dimensions={0} | all-to-all | bytes 65536 | tf_op jit(solution)/shard_map/all_to_all | solution.py:99
  230.2 0.5 broadcast.746
  230.7 0.7 reduce.6
  231.6 0.7 all_to_all.21
  (20 shorter events, 1.7 us)
Async XLA Ops:
  0.0 1.6 copy-start
  65.5 64.4 %copy-start.2 = (s32[2048]{0:T(1024)S(1)}, s32[2048]{0:T(1024)}, u32[]{:S(2)}) copy-start(s32[2048]{0:T(1024)} %param.12) | copy-start | bytes 24580
  176.0 14.9 %copy-start.3 = (s32[256]{0:T(256)S(1)}, s32[256]{0:T(256)}, u32[]{:S(2)}) copy-start(s32[256]{0:T(256)} %param.13) | copy-start | bytes 3076
  176.0 56.3 %copy-start.1 = (bf16[8,2,32,2048]{3,2,1,0:T(8,128)(2,1)S(1)}, bf16[8,2,32,2048]{3,2,1,0:T(8,128)(2,1)}, u32[]{:S(2)}) copy-start(bf16[8,2,32,2048]{3,2,1,0:T(8,128)(2,1)} %param.11) | copy-start | bytes 6291460
  177.3 9.0 %collective-permute-start = (f32[32,2048]{1,0:T(8,128)S(1)}, f32[32,2048]{1,0:T(8,128)S(1)}, u32[]{:S(2)}, u32[]{:S(2)}) collective-permute-start(f32[32,2048]{1,0:T(8,128)S(1)} %get-tuple-element.45), channel_id=1, source_target_pairs={{0,8},{8,16},{16,24},{24,32},{32,40},{40,48},{48,56},{56,64},{64,7... | collective-permute-start | bytes 786440 | tf_op jit(solution)/shard_map/ppermute | solution.py:13
  181.4 8.8 %collective-permute-start.1 = (f32[32,2048]{1,0:T(8,128)S(1)}, f32[32,2048]{1,0:T(8,128)S(1)}, u32[]{:S(2)}, u32[]{:S(2)}) collective-permute-start(f32[32,2048]{1,0:T(8,128)S(1)} %get-tuple-element.46), channel_id=1, source_target_pairs={{8,0},{16,8},{24,16},{32,24},{40,32},{48,40},{56,48},{64,56},{72,6... | collective-permute-start | bytes 786440 | tf_op jit(solution)/shard_map/ppermute | solution.py:13
where the time goes:
time: 233 us; the launch traced here: 232 us
  matrix products  129 us (55%)
  other arithmetic  48.1 us (21%)
  blocking collectives  33.9 us (15%)
  local copies, waits for them, and re-layouts  7.89 us (3%)
  waiting for transfers between devices  7.5 us (3%)
  starting transfers between devices  5.33 us (2%)
    dot_general x1, matrix products, batch_powers(): jnp.dot(stacked, sine_table, preferred_element_type=jnp.float32)  64.4 us
    dot_general x1, matrix products, batch_powers(): jnp.dot(stacked, cosine, preferred_element_type=jnp.float32)  63.9 us
    select_n x6, other arithmetic, walk_align(): current = jnp.where(taken, current[:, stride:], current[:, :-stride])  41 us
    all_to_all x1, blocking collectives, on_device(): lax.all_to_all(summed, 'dop', split_axis=1, concat_axis=0, tiled=True)  21.5 us
    all_to_all x1, blocking collectives, summed_on_arrival(): lax.all_to_all(tiles, axis, split_axis=0, concat_axis=0, tiled=True)  12.4 us
    ppermute x2, waiting for transfers between devices, from_behind(): lax.ppermute(value, axis, [(source, source + steps) for source in range(l...  7.5 us
    ppermute x2, starting transfers between devices, from_behind(): lax.ppermute(value, axis, [(source, source + steps) for source in range(l...  5.33 us
  transfers between devices with their start and end apart: 2, of which 2 were waited for; matrix products, arithmetic and copies ran while one was open for 0% of the time, Pallas kernels for 0%

commit v1 on v0

--- a/solution.py
+++ b/solution.py
@@ -96,7 +96,10 @@
     grouped = ordered.reshape(local_rows, dop_count, slow_count, band_rows).transpose(0, 2, 1, 3)
     grouped = grouped.reshape(local_rows, doppler_bins)
     summed = summed_on_arrival(grouped, "slow", 1)
-    result = lax.all_to_all(summed, "dop", split_axis=1, concat_axis=0, tiled=True)
+    size = lax.axis_size("dop")
+    blocks = jnp.stack(jnp.split(summed, size, axis=1), axis=0)
+    blocks = lax.all_to_all(blocks, "dop", split_axis=0, concat_axis=0)
+    result = jnp.concatenate(blocks, axis=0)
     return result.T
 
 

time: 233 us -> 235 us (level)
  no operation moved by 1% of the time
where the time goes in v1:
time: 235 us
  matrix products  129 us (55%)
  other arithmetic  48 us (20%)
  blocking collectives  33.9 us (14%)
  local copies, waits for them, and re-layouts  10.2 us (4%)
  waiting for transfers between devices  7.5 us (3%)
  starting transfers between devices  5.33 us (2%)
    dot_general x1, matrix products, batch_powers(): jnp.dot(stacked, sine_table, preferred_element_type=jnp.float32)  64.5 us
    dot_general x1, matrix products, batch_powers(): jnp.dot(stacked, cosine, preferred_element_type=jnp.float32)  63.9 us
    select_n x6, other arithmetic, walk_align(): current = jnp.where(taken, current[:, stride:], current[:, :-stride])  41 us
    all_to_all x1, blocking collectives, on_device(): blocks = lax.all_to_all(blocks, 'dop', split_axis=0, concat_axis=0)  21.5 us
    all_to_all x1, blocking collectives, summed_on_arrival(): lax.all_to_all(tiles, axis, split_axis=0, concat_axis=0, tiled=True)  12.4 us
    ppermute x2, waiting for transfers between devices, from_behind(): lax.ppermute(value, axis, [(source, source + steps) for source in range(l...  7.5 us
    ppermute x2, starting transfers between devices, from_behind(): lax.ppermute(value, axis, [(source, source + steps) for source in range(l...  5.33 us
  transfers between devices with their start and end apart: 2, of which 2 were waited for; matrix products, arithmetic and copies ran while one was open for 0% of the time, Pallas kernels for 0%

profile of v1, /device:TPU:1, one launch (start us, length us, event | category | flops | bytes accessed | tf_op | source)
XLA Modules:
  0.0 235.0 jit_solution(1564560835677232557)
XLA Ops:
  0.0 1.6 copy-done
  1.6 63.9 %fusion.7 = f32[2048,512]{0,1:T(8,128)} fusion(bf16[512,2048]{1,0:T(8,128)(2,1)S(1)} %bitcast.124), kind=kOutput, calls=%fused_computation.19 | convolution fusion | flops 4357881856 | bytes 6291456 | tf_op jit(solution)/shard_map/dot_general | solution.py:39
  65.5 64.5 %fusion.8 = f32[2048,512]{0,1:T(8,128)} fusion(bf16[512,2048]{1,0:T(8,128)(2,1)S(1)} %bitcast.123), kind=kOutput, calls=%fused_computation.20 | convolution fusion | flops 4357881856 | bytes 6291456 | tf_op jit(solution)/shard_map/dot_general | solution.py:42
  130.5 4.5 %fusion.15 = f32[8,32,2048]{2,1,0:T(8,128)S(1)} fusion(f32[8,2,32,2048]{3,2,1,0:T(8,128)} %bitcast.129, f32[8,2,32,2048]{3,2,1,0:T(8,128)} %bitcast.128), kind=kLoop, calls=%fused_computation.27 | loop fusion | flops 2621440 | bytes 10485760 | tf_op jit(solution)/shard_map/add | solution.py:47
  135.0 7.2 %fusion.6 = f32[8,222,2048]{2,1,0:T(8,128)} fusion(f32[8,32,2048]{2,1,0:T(8,128)S(1)} %fusion.15, pred[8,2048]{1,0:T(8,128)(4,1)S(1)} %get-tuple-element.83), kind=kLoop, calls=%fused_computation.13 | loop fusion | flops 3637248 | bytes 16662528 | tf_op jit(solution)/shard_map/jit(_where)/select_n | solution.py:58
  142.2 10.7 %slice_select_fusion = f32[8,220,2048]{2,1,0:T(8,128)S(1)} fusion(f32[8,222,2048]{2,1,0:T(8,128)} %fusion.6, pred[8,2048]{1,0:T(8,128)(4,1)S(1)} %get-tuple-element.85), kind=kLoop, calls=%fused_computation.14 | loop fusion | flops 3604480 | bytes 43270144 | tf_op jit(solution)/shard_map/jit(_where)/select_n | solution.py:58
  152.9 3.4 %slice_select_fusion.1 = f32[8,216,2048]{2,1,0:T(8,128)S(1)} fusion(f32[8,220,2048]{2,1,0:T(8,128)S(1)} %slice_select_fusion, pred[8,2048]{1,0:T(8,128)(4,1)S(1)} %get-tuple-element.81), kind=kLoop, calls=%fused_computation.15 | loop fusion | flops 3538944 | bytes 42483712 | tf_op jit(solution)/shard_map/jit(_where)/select_n | solution.py:58
  156.2 6.7 %slice_select_fusion.2 = f32[8,208,2048]{2,1,0:T(8,128)} fusion(f32[8,216,2048]{2,1,0:T(8,128)S(1)} %slice_select_fusion.1, pred[8,2048]{1,0:T(8,128)(4,1)S(1)} %get-tuple-element.84), kind=kLoop, calls=%fused_computation.16 | loop fusion | flops 3407872 | bytes 40910848 | tf_op jit(solution)/shard_map/jit(_where)/select_n | solution.py:58
  162.9 9.4 %slice_select_fusion.3 = f32[8,192,2048]{2,1,0:T(8,128)S(1)} fusion(f32[8,208,2048]{2,1,0:T(8,128)} %slice_select_fusion.2, pred[8,2048]{1,0:T(8,128)(4,1)S(1)} %get-tuple-element.82), kind=kLoop, calls=%fused_computation.17 | loop fusion | flops 3145728 | bytes 37765120 | tf_op jit(solution)/shard_map/jit(_where)/select_n | solution.py:58
  172.3 3.7 %slice_select_fusion.4 = f32[8,160,2048]{2,1,0:T(8,128)S(1)} fusion(f32[8,192,2048]{2,1,0:T(8,128)S(1)} %slice_select_fusion.3, pred[8,2048]{1,0:T(8,128)(4,1)S(1)} %get-tuple-element.80), kind=kLoop, calls=%fused_computation.18 | loop fusion | flops 2621440 | bytes 31473664 | tf_op jit(solution)/shard_map/jit(_where)/select_n | solution.py:58
  176.0 1.2 fusion.11
  177.3 4.0 %collective-permute-start = (f32[32,2048]{1,0:T(8,128)S(1)}, f32[32,2048]{1,0:T(8,128)S(1)}, u32[]{:S(2)}, u32[]{:S(2)}) collective-permute-start(f32[32,2048]{1,0:T(8,128)S(1)} %get-tuple-element.45), channel_id=1, source_target_pairs={{0,8},{8,16},{16,24},{24,32},{32,40},{40,48},{48,56},{56,64},{64,7... | collective-permute-start | bytes 786440 | tf_op jit(solution)/shard_map/ppermute | solution.py:13
  181.4 1.3 collective-permute-start.1
  182.7 3.7 %collective-permute-done = f32[32,2048]{1,0:T(8,128)S(1)} collective-permute-done((f32[32,2048]{1,0:T(8,128)S(1)}, f32[32,2048]{1,0:T(8,128)S(1)}, u32[]{:S(2)}, u32[]{:S(2)}) %collective-permute-start) | collective-permute-done | bytes 262176 | tf_op jit(solution)/shard_map/ppermute | solution.py:13
  186.3 3.8 %collective-permute-done.1 = f32[32,2048]{1,0:T(8,128)S(1)} collective-permute-done((f32[32,2048]{1,0:T(8,128)S(1)}, f32[32,2048]{1,0:T(8,128)S(1)}, u32[]{:S(2)}, u32[]{:S(2)}) %collective-permute-start.1) | collective-permute-done | bytes 262176 | tf_op jit(solution)/shard_map/ppermute | solution.py:13
  191.0 1.1 convolution_bitcast_fusion
  192.1 1.4 copy.105
  193.4 1.0 copy.146
  194.5 1.5 copy.107
  196.0 12.4 %all_to_all.10 = f32[8,32,256]{2,1,0:T(8,128)S(1)} all-to-all(f32[8,32,256]{2,1,0:T(8,128)S(1)} %copy.107), channel_id=1, replica_groups=mesh['dop'=32,'slow'=8] {'slow'}, dimensions={0} | all-to-all | bytes 524288 | tf_op jit(solution)/shard_map/all_to_all | solution.py:23
  211.3 21.5 %all_to_all.11 = f32[32,1,256]{2,1,0:T(1,128)S(1)} all-to-all(f32[32,1,256]{2,1,0:T(1,128)S(1)} %reshape.393), channel_id=1, replica_groups=mesh['dop'=32,'slow'=8] {'dop'}, dimensions={0} | all-to-all | bytes 65536 | tf_op jit(solution)/shard_map/all_to_all | solution.py:101
  232.9 0.5 broadcast.746
  233.4 0.7 reduce.6
  234.2 0.7 reshape.391
  (83 shorter events, 4.0 us)
Async XLA Ops:
  0.0 1.6 copy-start
  65.5 64.5 %copy-start.2 = (s32[2048]{0:T(1024)S(1)}, s32[2048]{0:T(1024)}, u32[]{:S(2)}) copy-start(s32[2048]{0:T(1024)} %param.12) | copy-start | bytes 24580
  176.0 14.9 %copy-start.3 = (s32[256]{0:T(256)S(1)}, s32[256]{0:T(256)}, u32[]{:S(2)}) copy-start(s32[256]{0:T(256)} %param.13) | copy-start | bytes 3076
  176.0 58.9 %copy-start.1 = (bf16[8,2,32,2048]{3,2,1,0:T(8,128)(2,1)S(1)}, bf16[8,2,32,2048]{3,2,1,0:T(8,128)(2,1)}, u32[]{:S(2)}) copy-start(bf16[8,2,32,2048]{3,2,1,0:T(8,128)(2,1)} %param.11) | copy-start | bytes 6291460
  177.3 9.0 %collective-permute-start = (f32[32,2048]{1,0:T(8,128)S(1)}, f32[32,2048]{1,0:T(8,128)S(1)}, u32[]{:S(2)}, u32[]{:S(2)}) collective-permute-start(f32[32,2048]{1,0:T(8,128)S(1)} %get-tuple-element.45), channel_id=1, source_target_pairs={{0,8},{8,16},{16,24},{24,32},{32,40},{40,48},{48,56},{56,64},{64,7... | collective-permute-start | bytes 786440 | tf_op jit(solution)/shard_map/ppermute | solution.py:13
  181.4 8.8 %collective-permute-start.1 = (f32[32,2048]{1,0:T(8,128)S(1)}, f32[32,2048]{1,0:T(8,128)S(1)}, u32[]{:S(2)}, u32[]{:S(2)}) collective-permute-start(f32[32,2048]{1,0:T(8,128)S(1)} %get-tuple-element.46), channel_id=1, source_target_pairs={{8,0},{16,8},{24,16},{32,24},{40,32},{48,40},{56,48},{64,56},{72,6... | collective-permute-start | bytes 786440 | tf_op jit(solution)/shard_map/ppermute | solution.py:13
